TPU v7x, 32 devices: a whole 2x2x4 slice. The times are simulated.
32 devices in a mesh: dp: 16 (over z, x, core), tensor: 2 (over y).
Axes of the slice: x: 2, y: 2, z: 4, core: 2. Of those that a mesh axis runs over, the one named last changes fastest.
Arguments:
- hidden: bfloat16 [5120, 18432], P('dp', 'tensor'), may hold values from -6 to 6
- fixed_down_weight: bfloat16 [18432, 4608], P('tensor', 'dp'), may hold values from -4 to 4
- lowrank_factor_b: bfloat16 [18432, 16], P('tensor'), may hold values from -0.046875 to 0.046875
- lowrank_factor_a: bfloat16 [16, 4608], P(None, 'dp'), may hold values from -1.5 to 1.5
- magnitude: float32 [4608], P('tensor'), may hold values from 0.5 to 2
- cotangent: bfloat16 [5120, 4608], P('dp', 'tensor'), may hold values from -0.083496094 to 0.083496094
Outputs:
- mixed: bfloat16 [5120, 4608], P('dp', 'tensor')
- gradient_column_scale: float32 [4608], P(('tensor', 'dp'))
- gradient_factor_a: float32 [16, 4608], P(None, ('tensor', 'dp'))
- gradient_factor_b: float32 [18432, 16], P(('tensor', 'dp'))
All inputs are finite; a program needn't handle non-finite values.
Results may differ from a plain program's by a relative error of at most 0.0054.
Values may be sent and summed in bfloat16 or wider, within the bound.
No kernel may reach another device: no remote copies, remote signals or barrier semaphores. Data moves between devices by JAX's collectives and lax.ppermute only.
A program may use at most 192 MiB of HBM per device.

v0:
```python
import jax
import jax.numpy as jnp
from jax import lax
from jax.sharding import PartitionSpec as P


def body(hidden, fixed_down_weight, lowrank_factor_b, lowrank_factor_a, magnitude, cotangent):
    out_cols = magnitude.shape[0]
    own = lax.axis_index("tensor")
    lowrank_portion = jnp.dot(hidden, lowrank_factor_b, preferred_element_type=jnp.float32)
    combined_weight = fixed_down_weight.astype(jnp.float32) + jnp.dot(
        lowrank_factor_b, lowrank_factor_a, preferred_element_type=jnp.float32
    )
    local_sq = jnp.sum(combined_weight * combined_weight, axis=0)
    low_full, block_sq = lax.psum((lowrank_portion, local_sq), "tensor")
    col_sq = lax.all_gather(block_sq, "dp", axis=0, tiled=True)
    sq_len = 1
    weight_shape = (1, 1)
    squares = jnp.zeros((sq_len,), jnp.float32)
    full_w = jnp.zeros(weight_shape, jnp.bfloat16)
    w_piece = lax.all_gather(fixed_down_weight, "dp", axis=1, tiled=True)
    factor_a_slice = lax.all_gather(lowrank_factor_a, "dp", axis=1, tiled=True)
    products = jnp.dot(hidden, w_piece, preferred_element_type=jnp.float32)
    full_a = factor_a_slice
    products, squares, full_a, full_w = (products, squares, full_a, full_w)
    column_norm_values = jnp.sqrt(col_sq + 1e-06)
    own_norms = lax.dynamic_slice_in_dim(column_norm_values, own * out_cols, out_cols, 0)
    scale = magnitude / own_norms
    lowrank_block_update = low_full.astype(jnp.bfloat16)
    summed = lax.psum_scatter(products, "tensor", scatter_dimension=1, tiled=True)
    own_a = lax.dynamic_slice_in_dim(full_a, own * out_cols, out_cols, 1)
    prenorm_output = summed + jnp.dot(
        lowrank_block_update, own_a, preferred_element_type=jnp.float32
    )
    mixed = (prenorm_output * scale).astype(jnp.bfloat16)
    cot = cotangent.astype(jnp.float32)
    mag_part = jnp.sum(cot * prenorm_output, axis=0) / own_norms
    prenorm_gradient_b = (cot * scale).astype(jnp.bfloat16)
    factor_a_portion = jnp.dot(
        lowrank_block_update.T, prenorm_gradient_b, preferred_element_type=jnp.float32
    )
    back_part = jnp.dot(prenorm_gradient_b, own_a.T, preferred_element_type=jnp.float32)
    backward_factor_b = lax.psum(back_part, "tensor").astype(jnp.bfloat16)
    b_part = jnp.dot(hidden.T, backward_factor_b, preferred_element_type=jnp.float32)
    gradient_column_scale, gradient_factor_b = (
        lax.psum_scatter(mag_part, "dp", scatter_dimension=0, tiled=True),
        lax.psum_scatter(b_part, "dp", scatter_dimension=0, tiled=True),
    )
    gradient_factor_a = lax.psum_scatter(factor_a_portion, "dp", scatter_dimension=1, tiled=True)
    return (mixed, gradient_column_scale, gradient_factor_a, gradient_factor_b)


def solution(mesh):
    return jax.shard_map(
        body,
        mesh=mesh,
        in_specs=(
            P("dp", "tensor"),
            P("tensor", "dp"),
            P("tensor", None),
            P(None, "dp"),
            P("tensor"),
            P("dp", "tensor"),
        ),
        out_specs=(
            P("dp", "tensor"),
            P(("tensor", "dp")),
            P(None, ("tensor", "dp")),
            P(("tensor", "dp"), None),
        ),
        check_vma=False,
    )
```

profile of v0, /device:TPU:0, one launch (start us, length us, event | category | flops | bytes accessed | tf_op | source)
XLA Modules:
  0.0 711.5 jit_solution(8600215113139559798)
XLA Ops:
  7.2 0.0 copy-start
  7.2 0.0 copy-start.4
  7.2 0.0 copy-start.2
  7.2 0.0 all-gather.3.cloned.1.call-start
  7.2 0.7 all-gather.3.cloned.1.call-update
  7.9 0.0 reduce-scatter.10.cloned.1.call-start
  8.0 0.0 copy-done.2
  8.0 24.5 %all-gather = bf16[16,288,16]{1,2,0:T(8,128)(2,1)S(1)} all-gather(bf16[1,288,16]{1,2,0:T(8,128)(2,1)S(1)} %bitcast.24), channel_id=1, replica_groups=mesh['dp'=16,'tensor'=2] {'dp'}, dimensions={0}, use_global_device_ids=true | all-gather | bytes 156672 | tf_op jit(solution)/shard_map/all_gather | solution.py:22
  32.6 0.2 reshape.13
  32.8 0.0 copy-done.4
  32.8 0.6 fusion.17
  34.0 0.0 copy-done
  34.0 0.0 copy-start.3
  34.0 0.0 copy-start.1
  34.1 4.4 fusion.3
  38.4 4.9 psum.22
  43.4 0.2 dynamic-update-slice
  43.6 61.0 %all-reduce = f32[4608]{0:T(1024)S(1)} all-reduce(f32[4608]{0:T(1024)S(1)} %dynamic-update-slice), channel_id=1, replica_groups=mesh['dp'=16,'tensor'=2] {'dp'}, use_global_device_ids=true, to_apply=%add | all-reduce | flops 4608 | bytes 36864
  104.6 0.0 copy-done.3
  104.6 0.1 fusion.11
  104.7 0.0 copy-done.1
  104.7 0.5 fusion.4
  105.2 4.3 fusion.19
  109.6 8.7 %all-reduce.2 = (bf16[320,16]{0,1:T(8,128)(2,1)S(1)}, bf16[320,16]{0,1:T(8,128)(2,1)S(1)}) all-reduce(f32[320,16]{0,1:T(8,128)S(1)} %fusion.19, f32[320,16]{0,1:T(8,128)S(1)} %fusion.4), channel_id=1, replica_groups=mesh['dp'=16,'tensor'=2] {'tensor'}, use_global_device_ids=true, to_apply=%region_1.0 | all-reduce | flops 10240 | bytes 61440 | tf_op jit(solution)/shard_map/psum | solution.py:15
  118.3 1.8 convolution_bitcast_fusion.1
  120.1 0.0 reduce-scatter.10.cloned.1.call-update
  120.1 0.0 reduce-scatter.12.cloned.1.call-start
  120.2 3.7 convolution_bitcast_fusion
  123.9 2.9 copy.14
  126.8 0.0 reduce-scatter.12.cloned.1.call-update
  126.8 0.0 reduce-scatter.8.cloned.1.call-start
  126.8 296.7 %all-gather.3.cloned.1.call-done = bf16[9216,4608]{0,1:T(8,128)(2,1)} async-done(((bf16[9216,288]{0,1:T(8,128)(2,1)}), bf16[9216,4608]{0,1:T(8,128)(2,1)}) %all-gather.3.cloned.1.call-update) | async-done | bytes 84934672 | tf_op jit(solution)/shard_map/all_gather | solution.py:21
  423.6 40.2 %fusion.18 = f32[320,4608]{1,0:T(8,128)} fusion(bf16[320,9216]{1,0:T(8,128)(2,1)} %param.6, bf16[9216,4608]{0,1:T(8,128)(2,1)} %all-gather.3.cloned.1.call-done), kind=kOutput, calls=%fused_computation.24 | convolution fusion | flops 27179089920 | bytes 96731136 | tf_op jit(solution)/shard_map/dot_general | solution.py:23
  463.8 0.0 reduce-scatter.8.cloned.1.call-update
  464.4 22.3 %reduce-scatter.10.cloned.1.call-done = f32[144,16]{1,0:T(8,128)} async-done(((f32[2304,16]{1,0:T(8,128)}), f32[144,16]{1,0:T(8,128)}) %reduce-scatter.10.cloned.1.call-update) | async-done | bytes 9232
  486.7 1.6 copy.13
  488.3 77.0 %reduce-scatter.12.cloned.1.call-done = f32[576,16]{1,0:T(8,128)} async-done(((f32[9216,16]{1,0:T(8,128)}), f32[576,16]{1,0:T(8,128)}) %reduce-scatter.12.cloned.1.call-update) | async-done | bytes 36880
  565.2 1.7 copy.15
  566.9 72.6 %reduce-scatter.8.cloned.1.call-done = f32[320,2304]{1,0:T(8,128)} async-done(((f32[320,4608]{1,0:T(8,128)}), f32[320,2304]{1,0:T(8,128)}) %reduce-scatter.8.cloned.1.call-update) | async-done | bytes 2949136 | tf_op jit(solution)/shard_map/reduce_scatter | solution.py:30
  639.6 3.7 fusion.1
  643.3 0.1 fusion.12
  643.3 61.0 %all-reduce.1 = f32[2304]{0:T(1024)S(1)} all-reduce(f32[2304]{0:T(1024)S(1)} %fusion.12), channel_id=3, replica_groups=mesh['dp'=16,'tensor'=2] {'dp'}, use_global_device_ids=true, to_apply=%region_5.0.clone | all-reduce | flops 2304 | bytes 18432
  704.4 0.6 dynamic-slice.3
  (2 shorter events, 0.0 us)
Async XLA Ops:
  7.2 26.9 %copy-start = (bf16[9216,16]{0,1:T(8,128)(2,1)S(1)}, bf16[9216,16]{0,1:T(8,128)(2,1)}, u32[]{:S(2)}) copy-start(bf16[9216,16]{0,1:T(8,128)(2,1)} %param.8) | copy-start | bytes 884740
  7.2 25.6 %copy-start.4 = (u32[32]{0:T(128)S(1)}, u32[32]{0:T(128)}, u32[]{:S(2)}) copy-start(u32[32]{0:T(128)} %constant.16) | copy-start | bytes 388
  7.2 0.8 copy-start.2
  7.2 416.4 %all-gather.3.cloned.1.call-start = ((), (), s32[]{:S(2)}) async-start(), calls=%async_computation.3 | async-start | bytes 90243072 | tf_op jit(solution)/shard_map/all_gather | solution.py:21
  7.9 478.8 %reduce-scatter.10.cloned.1.call-start = ((), (), s32[]{:S(2)}) async-start(), calls=%async_computation.5 | async-start | bytes 1253376
  34.0 70.6 %copy-start.3 = (f32[2304]{0:T(1024)S(1)}, f32[2304]{0:T(1024)}, u32[]{:S(2)}) copy-start(f32[2304]{0:T(1024)} %param.10) | copy-start | bytes 27652
  34.0 70.7 %copy-start.1 = (bf16[320,2304]{1,0:T(8,128)(2,1)S(1)}, bf16[320,2304]{1,0:T(8,128)(2,1)}, u32[]{:S(2)}) copy-start(bf16[320,2304]{1,0:T(8,128)(2,1)} %param.11) | copy-start | bytes 4423684
  120.1 445.1 %reduce-scatter.12.cloned.1.call-start = ((), (), s32[]{:S(2)}) async-start(), calls=%async_computation.6 | async-start | bytes 5013504
  126.8 512.8 %reduce-scatter.8.cloned.1.call-start = ((), (), s32[]{:S(2)}) async-start(), calls=%async_computation.4 | async-start | bytes 8847360 | tf_op jit(solution)/shard_map/reduce_scatter | solution.py:30
Sparse Core Ops, SparseCore 0:
  9.6 413.9 all-gather.2
  427.7 58.9 reduce-scatter.9
  490.6 74.6 reduce-scatter.11
  567.4 72.1 reduce-scatter.7
where the time goes:
time: 712 us
  waiting for transfers between devices  469 us (66%)
  blocking collectives  160 us (22%)
  matrix products  58.6 us (8%)
  between operations  15.2 us (2%)
  local copies, waits for them, and re-layouts  7.9 us (1%)
    all_gather x1, waiting for transfers between devices, body(): w_piece = lax.all_gather(fixed_down_weight, 'dp', axis=1, tiled=True)  297 us
    unnamed x2, blocking collectives  122 us
    unnamed x6, waiting for transfers between devices  100 us
    reduce_scatter x1, waiting for transfers between devices, body(): lax.psum_scatter(products, 'tensor', scatter_dimension=1, tiled=True)  72.6 us
    dot_general x1, matrix products, body(): products = jnp.dot(hidden, w_piece, preferred_element_type=jnp.float32)  40.2 us
    all_gather x1, blocking collectives, body(): factor_a_slice = lax.all_gather(lowrank_factor_a, 'dp', axis=1, tiled=True)  24.5 us
  transfers between devices with their start and end apart: 4, of which 4 were waited for; matrix products, arithmetic and copies ran while one was open for 9% of the time, Pallas kernels for 0%

commit v1 on v0

--- a/solution.py
+++ b/solution.py
@@ -2,6 +2,34 @@
 import jax.numpy as jnp
 from jax import lax
 from jax.sharding import PartitionSpec as P
+
+
+def enter_ranges_all(obj):
+    frames = []
+    taken_in, now, q_next = (lax.axis_size("dp"), lax.axis_index("dp"), obj.shape[1])
+    for it, nth in enumerate(obj.shape):
+        frames.append(nth * taken_in if it == 1 else nth)
+    step_out = right_arr = obj
+    left_arr = lax.dynamic_update_slice_in_dim(
+        jnp.zeros(frames, obj.dtype), obj, now * q_next, axis=1
+    )
+    for to_i in [*range(1, taken_in // 2 + 1)]:
+        kept_rows = []
+        for it in tuple(range(taken_in)):
+            kept_rows.append((it, (it + 1) % taken_in))
+        step_out = lax.ppermute(step_out, "dp", kept_rows)
+        left_arr = lax.dynamic_update_slice_in_dim(
+            left_arr, step_out, (now - to_i) % taken_in * q_next, axis=1
+        )
+        if 2 * to_i < taken_in:
+            trail = []
+            for it in tuple(range(taken_in)):
+                trail.append((it, (it - 1) % taken_in))
+            right_arr = lax.ppermute(right_arr, "dp", trail)
+            left_arr = lax.dynamic_update_slice_in_dim(
+                left_arr, right_arr, (now + to_i) % taken_in * q_next, axis=1
+            )
+    return left_arr
 
 
 def body(hidden, fixed_down_weight, lowrank_factor_b, lowrank_factor_a, magnitude, cotangent):
@@ -18,7 +46,7 @@
     weight_shape = (1, 1)
     squares = jnp.zeros((sq_len,), jnp.float32)
     full_w = jnp.zeros(weight_shape, jnp.bfloat16)
-    w_piece = lax.all_gather(fixed_down_weight, "dp", axis=1, tiled=True)
+    w_piece = enter_ranges_all(fixed_down_weight)
     factor_a_slice = lax.all_gather(lowrank_factor_a, "dp", axis=1, tiled=True)
     products = jnp.dot(hidden, w_piece, preferred_element_type=jnp.float32)
     full_a = factor_a_slice

time: 712 us -> 1180 us (1.66)
  starting transfers between devices: 0.16 us -> 532 us
  waiting for transfers between devices: 469 us -> 265 us
  local copies, waits for them, and re-layouts: 7.9 us -> 103 us
  blocking collectives: 160 us -> 206 us
    ppermute x0 -> x15, starting transfers between devices: none -> 532 us  [the longest x8 517 us: enter_ranges_all(): step_out = lax.ppermute(step_out, 'dp', kept_rows)]
    all_gather x1 -> x0, waiting for transfers between devices: 297 us -> none  [body(): w_piece = lax.all_gather(fixed_down_weight, 'dp', axis=1, tiled=True)]
    ppermute x0 -> x15, waiting for transfers between devices: none -> 162 us  [the longest x8 162 us: enter_ranges_all(): step_out = lax.ppermute(step_out, 'dp', kept_rows)]
    unnamed x6 -> x5, waiting for transfers between devices: 100 us -> 0.07 us
    dynamic_update_slice x0 -> x16, local copies, waits for them, and re-layouts: none -> 64.3 us  [the longest x8 32.4 us: enter_ranges_all(): lax.dynamic_update_slice_in_dim(left_arr, step_out, (now - to_i) % taken_...]
    all_gather x1, blocking collectives: 24.5 us -> 73.3 us  [body(): factor_a_slice = lax.all_gather(lowrank_factor_a, 'dp', axis=1, tiled=True)]
    reduce_scatter x1, waiting for transfers between devices: 72.6 us -> 103 us  [body(): lax.psum_scatter(products, 'tensor', scatter_dimension=1, tiled=True)]
    broadcast_in_dim x0 -> x1, local copies, waits for them, and re-layouts: none -> 27.8 us  [enter_ranges_all(): jnp.zeros(frames, obj.dtype)]
  transfers between devices with their start and end apart: 4 -> 18, of which waited for: 4 -> 8; matrix products, arithmetic and copies ran while one was open for 9% -> 13% of each run, Pallas kernels for 0% -> 0%
where the time goes in v1:
time: 1180 us
  starting transfers between devices  532 us (45%)
  waiting for transfers between devices  265 us (22%)
  blocking collectives  206 us (17%)
  local copies, waits for them, and re-layouts  103 us (9%)
  matrix products  56.3 us (5%)
  between operations  15.6 us (1%)
    ppermute x8, starting transfers between devices, enter_ranges_all(): step_out = lax.ppermute(step_out, 'dp', kept_rows)  517 us
    ppermute x8, waiting for transfers between devices, enter_ranges_all(): step_out = lax.ppermute(step_out, 'dp', kept_rows)  162 us
    unnamed x2, blocking collectives  119 us
    reduce_scatter x1, waiting for transfers between devices, body(): lax.psum_scatter(products, 'tensor', scatter_dimension=1, tiled=True)  103 us
    all_gather x1, blocking collectives, body(): factor_a_slice = lax.all_gather(lowrank_factor_a, 'dp', axis=1, tiled=True)  73.3 us
    dot_general x1, matrix products, body(): products = jnp.dot(hidden, w_piece, preferred_element_type=jnp.float32)  41.1 us
    dynamic_update_slice x8, local copies, waits for them, and re-layouts, enter_ranges_all(): lax.dynamic_update_slice_in_dim(left_arr, step_out, (now - to_i) % taken_...  32.4 us
    dynamic_update_slice x7, local copies, waits for them, and re-layouts, enter_ranges_all(): lax.dynamic_update_slice_in_dim(left_arr, right_arr, (now + to_i) % taken...  29.2 us
  transfers between devices with their start and end apart: 18, of which 8 were waited for; matrix products, arithmetic and copies ran while one was open for 13% of the time, Pallas kernels for 0%

profile of v1, /device:TPU:0, one launch (start us, length us, event | category | flops | bytes accessed | tf_op | source)
XLA Modules:
  0.0 1182.2 jit_solution(4994721848121186545)
XLA Ops:
  7.2 0.0 reduce-scatter.10.cloned.1.call-start
  7.2 0.5 collective-permute-start
  7.8 5.0 collective-permute-start.1
  12.8 58.4 %collective-permute-done = bf16[9216,288]{0,1:T(8,128)(2,1)S(1)} collective-permute-done((bf16[9216,288]{0,1:T(8,128)(2,1)}, bf16[9216,288]{0,1:T(8,128)(2,1)S(1)}, u32[]{:S(2)}, u32[]{:S(2)}) %collective-permute-start) | collective-permute-done | bytes 5308448 | tf_op jit(solution)/shard_map/ppermute | solution.py:20
  71.2 53.8 %collective-permute-start.2 = (bf16[9216,288]{0,1:T(8,128)(2,1)S(1)}, bf16[9216,288]{0,1:T(8,128)(2,1)S(1)}, u32[]{:S(2)}, u32[]{:S(2)}) collective-permute-start(bf16[9216,288]{0,1:T(8,128)(2,1)S(1)} %collective-permute-done), channel_id=1, source_target_pairs={{0,2},{2,4},{4,6},{6,8},{8,10},{10,12},{12,14},{14,16},{16,18},{18... | collective-permute-start | bytes 15925256 | tf_op jit(solution)/shard_map/ppermute | solution.py:20
  125.0 8.9 collective-permute-done.2
  133.8 107.1 %collective-permute-start.4 = (bf16[9216,288]{0,1:T(8,128)(2,1)S(1)}, bf16[9216,288]{0,1:T(8,128)(2,1)S(1)}, u32[]{:S(2)}, u32[]{:S(2)}) collective-permute-start(bf16[9216,288]{0,1:T(8,128)(2,1)S(1)} %collective-permute-done.2), channel_id=1, source_target_pairs={{0,2},{2,4},{4,6},{6,8},{8,10},{10,12},{12,14},{14,16},{16,18},{18... | collective-permute-start | bytes 15925256 | tf_op jit(solution)/shard_map/ppermute | solution.py:20
  240.9 8.4 collective-permute-done.4
  249.3 2.3 copy-done.3
  251.6 107.6 %collective-permute-start.6 = (bf16[9216,288]{0,1:T(8,128)(2,1)S(1)}, bf16[9216,288]{0,1:T(8,128)(2,1)}, u32[]{:S(2)}, u32[]{:S(2)}) collective-permute-start(bf16[9216,288]{0,1:T(8,128)(2,1)S(1)} %collective-permute-done.4), channel_id=1, source_target_pairs={{0,2},{2,4},{4,6},{6,8},{8,10},{10,12},{12,14},{14,16},{16,18},{18... | collective-permute-start | bytes 15925256 | tf_op jit(solution)/shard_map/ppermute | solution.py:20
  359.2 8.5 collective-permute-done.6
  367.8 107.7 %collective-permute-start.8 = (bf16[9216,288]{0,1:T(8,128)(2,1)}, bf16[9216,288]{0,1:T(8,128)(2,1)}, u32[]{:S(2)}, u32[]{:S(2)}) collective-permute-start(bf16[9216,288]{0,1:T(8,128)(2,1)} %collective-permute-done.6), channel_id=1, source_target_pairs={{0,2},{2,4},{4,6},{6,8},{8,10},{10,12},{12,14},{14,16},{16,18},{18... | collective-permute-start | bytes 15925256 | tf_op jit(solution)/shard_map/ppermute | solution.py:20
  475.4 73.3 %all-gather = bf16[16,288,16]{1,2,0:T(8,128)(2,1)S(1)} all-gather(bf16[1,288,16]{1,2,0:T(8,128)(2,1)} %bitcast.34), channel_id=1, replica_groups=mesh['dp'=16,'tensor'=2] {'dp'}, dimensions={0}, use_global_device_ids=true | all-gather | bytes 156672 | tf_op jit(solution)/shard_map/all_gather | solution.py:50
  548.8 0.2 reshape.13
  549.0 1.3 fusion.18
  551.0 4.3 fusion.3
  555.3 5.1 psum.22
  560.3 0.2 dynamic-update-slice
  560.6 57.6 %all-reduce = f32[4608]{0:T(1024)S(1)} all-reduce(f32[4608]{0:T(1024)S(1)} %dynamic-update-slice), channel_id=1, replica_groups=mesh['dp'=16,'tensor'=2] {'dp'}, use_global_device_ids=true, to_apply=%add | all-reduce | flops 4608 | bytes 36864
  618.2 0.1 fusion.12
  618.3 4.3 fusion.19
  622.6 0.0 collective-permute-start.9
  622.6 0.5 fusion.4
  623.1 8.6 all-reduce.2
  631.8 1.8 convolution_bitcast_fusion.2
  633.6 0.0 reduce-scatter.12.cloned.1.call-start
  633.7 3.7 convolution_bitcast_fusion
  637.4 3.0 copy.14
  640.5 0.0 reduce-scatter.8.cloned.1.call-start
  640.8 0.1 collective-permute-start.10
  640.9 27.8 %broadcast_in_dim.2 = bf16[9216,4608]{0,1:T(8,128)(2,1)} broadcast(bf16[]{:T(256)} %constant.95.clone.1), dimensions={} | broadcast | bytes 84934656 | tf_op jit(solution)/shard_map/broadcast_in_dim | solution.py:14
  668.7 2.7 constant_dynamic-update-slice_fusion.15
  671.4 5.7 constant_dynamic-update-slice_fusion.14
  677.1 5.5 constant_dynamic-update-slice_fusion.13
  682.6 3.0 constant_dynamic-update-slice_fusion.12
  685.7 3.0 collective-permute-start.11
  688.6 2.7 constant_dynamic-update-slice_fusion.11
  691.3 17.2 %collective-permute-done.10 = bf16[9216,288]{0,1:T(8,128)(2,1)} collective-permute-done((bf16[9216,288]{0,1:T(8,128)(2,1)}, bf16[9216,288]{0,1:T(8,128)(2,1)}, u32[]{:S(2)}, u32[]{:S(2)}) %collective-permute-start.10) | collective-permute-done | bytes 5308448 | tf_op jit(solution)/shard_map/ppermute | solution.py:20
  708.5 83.3 %collective-permute-start.12 = (bf16[9216,288]{0,1:T(8,128)(2,1)}, bf16[9216,288]{0,1:T(8,128)(2,1)S(1)}, u32[]{:S(2)}, u32[]{:S(2)}) collective-permute-start(bf16[9216,288]{0,1:T(8,128)(2,1)} %collective-permute-done.10), channel_id=1, source_target_pairs={{0,2},{2,4},{4,6},{6,8},{8,10},{10,12},{12,14},{14,16},{16,18},{18... | collective-permute-start | bytes 15925256 | tf_op jit(solution)/shard_map/ppermute | solution.py:20
  791.8 2.7 constant_dynamic-update-slice_fusion.10
  794.5 5.2 constant_dynamic-update-slice_fusion.9
  799.7 5.2 constant_dynamic-update-slice_fusion.8
  804.9 5.2 constant_dynamic-update-slice_fusion.7
  810.1 7.2 collective-permute-start.13
  817.3 5.2 constant_dynamic-update-slice_fusion.6
  822.6 45.4 %collective-permute-done.12 = bf16[9216,288]{0,1:T(8,128)(2,1)S(1)} collective-permute-done((bf16[9216,288]{0,1:T(8,128)(2,1)}, bf16[9216,288]{0,1:T(8,128)(2,1)S(1)}, u32[]{:S(2)}, u32[]{:S(2)}) %collective-permute-start.12) | collective-permute-done | bytes 5308448 | tf_op jit(solution)/shard_map/ppermute | solution.py:20
  868.0 56.6 %collective-permute-start.14 = (bf16[9216,288]{0,1:T(8,128)(2,1)S(1)}, bf16[9216,288]{0,1:T(8,128)(2,1)S(1)}, u32[]{:S(2)}, u32[]{:S(2)}) collective-permute-start(bf16[9216,288]{0,1:T(8,128)(2,1)S(1)} %collective-permute-done.12), channel_id=1, source_target_pairs={{0,2},{2,4},{4,6},{6,8},{8,10},{10,12},{12,14},{14,16},{16,18},{18... | collective-permute-start | bytes 15925256 | tf_op jit(solution)/shard_map/ppermute | solution.py:20
  924.6 5.2 constant_dynamic-update-slice_fusion.5
  929.9 5.1 constant_dynamic-update-slice_fusion.4
  935.0 2.7 constant_dynamic-update-slice_fusion.3
  937.8 2.6 constant_dynamic-update-slice_fusion.2
  940.4 2.7 constant_dynamic-update-slice_fusion.1
  943.1 15.5 %collective-permute-done.14 = bf16[9216,288]{0,1:T(8,128)(2,1)S(1)} collective-permute-done((bf16[9216,288]{0,1:T(8,128)(2,1)S(1)}, bf16[9216,288]{0,1:T(8,128)(2,1)S(1)}, u32[]{:S(2)}, u32[]{:S(2)}) %collective-permute-start.14) | collective-permute-done | bytes 5308448 | tf_op jit(solution)/shard_map/ppermute | solution.py:20
  958.6 2.8 constant_dynamic-update-slice_fusion
  961.3 41.1 %convolution_bitcast_fusion.1 = f32[320,4608]{1,0:T(8,128)} fusion(bf16[9216,4608]{0,1:T(8,128)(2,1)} %constant_dynamic-update-slice_fusion, bf16[320,9216]{1,0:T(8,128)(2,1)} %param.6), kind=kOutput, calls=%fused_computation.3 | convolution fusion | flops 27179089920 | bytes 96731136 | tf_op jit(solution)/shard_map/dot_general | solution.py:51
  1003.1 0.6 fusion.7
  1003.7 0.0 reduce-scatter.10.cloned.1.call-done
  1003.7 1.6 copy.13
  1005.3 1.7 copy.15
  1007.0 103.0 %reduce-scatter.8.cloned.1.call-done = f32[320,2304]{1,0:T(8,128)} async-done(((f32[320,4608]{1,0:T(8,128)}), f32[320,2304]{1,0:T(8,128)}) %reduce-scatter.8.cloned.1.call-update) | async-done | bytes 2949136 | tf_op jit(solution)/shard_map/reduce_scatter | solution.py:58
  1110.0 3.9 fusion.1
  1113.9 0.1 fusion.13
  1114.0 61.0 %all-reduce.1 = f32[2304]{0:T(1024)S(1)} all-reduce(f32[2304]{0:T(1024)S(1)} %fusion.13), channel_id=3, replica_groups=mesh['dp'=16,'tensor'=2] {'dp'}, use_global_device_ids=true, to_apply=%region_5.6.clone | all-reduce | flops 2304 | bytes 18432
  1175.0 0.6 dynamic-slice.3
  (54 shorter events, 0.2 us)
Async XLA Ops:
  7.2 543.8 %copy-start = (bf16[9216,16]{0,1:T(8,128)(2,1)S(1)}, bf16[9216,16]{0,1:T(8,128)(2,1)}, u32[]{:S(2)}) copy-start(bf16[9216,16]{0,1:T(8,128)(2,1)} %param.8) | copy-start | bytes 884740
  7.2 996.6 %reduce-scatter.10.cloned.1.call-start = ((), (), s32[]{:S(2)}) async-start(), calls=%async_computation.4 | async-start | bytes 1253376
  7.2 63.9 %collective-permute-start = (bf16[9216,288]{0,1:T(8,128)(2,1)}, bf16[9216,288]{0,1:T(8,128)(2,1)S(1)}, u32[]{:S(2)}, u32[]{:S(2)}) collective-permute-start(bf16[9216,288]{0,1:T(8,128)(2,1)} %param.7), channel_id=1, source_target_pairs={{0,2},{2,4},{4,6},{6,8},{8,10},{10,12},{12,14},{14,16},{16,18},{18... | collective-permute-start | bytes 15925256 | tf_op jit(solution)/shard_map/ppermute | solution.py:20
  7.8 117.2 %collective-permute-start.1 = (bf16[9216,288]{0,1:T(8,128)(2,1)}, bf16[9216,288]{0,1:T(8,128)(2,1)S(1)}, u32[]{:S(2)}, u32[]{:S(2)}) collective-permute-start(bf16[9216,288]{0,1:T(8,128)(2,1)} %param.7), channel_id=1, source_target_pairs={{0,30},{2,0},{4,2},{6,4},{8,6},{10,8},{12,10},{14,12},{16,14},{18,... | collective-permute-start | bytes 15925256 | tf_op jit(solution)/shard_map/ppermute | solution.py:28
  71.2 53.8 %copy-start.5 = (bf16[9216,288]{0,1:T(8,128)(2,1)}, bf16[9216,288]{0,1:T(8,128)(2,1)S(1)}, u32[]{:S(2)}) copy-start(bf16[9216,288]{0,1:T(8,128)(2,1)S(1)} %collective-permute-done) | copy-start | bytes 15925252
  71.2 62.7 %collective-permute-start.2 = (bf16[9216,288]{0,1:T(8,128)(2,1)S(1)}, bf16[9216,288]{0,1:T(8,128)(2,1)S(1)}, u32[]{:S(2)}, u32[]{:S(2)}) collective-permute-start(bf16[9216,288]{0,1:T(8,128)(2,1)S(1)} %collective-permute-done), channel_id=1, source_target_pairs={{0,2},{2,4},{4,6},{6,8},{8,10},{10,12},{12,14},{14,16},{16,18},{18... | collective-permute-start | bytes 15925256 | tf_op jit(solution)/shard_map/ppermute | solution.py:20
  124.9 350.5 %copy-start.6 = (bf16[9216,288]{0,1:T(8,128)(2,1)}, bf16[9216,288]{0,1:T(8,128)(2,1)S(1)}, u32[]{:S(2)}) copy-start(bf16[9216,288]{0,1:T(8,128)(2,1)S(1)} %collective-permute-done.1) | copy-start | bytes 15925252
  125.0 116.0 %collective-permute-start.3 = (bf16[9216,288]{0,1:T(8,128)(2,1)S(1)}, bf16[9216,288]{0,1:T(8,128)(2,1)S(1)}, u32[]{:S(2)}, u32[]{:S(2)}) collective-permute-start(bf16[9216,288]{0,1:T(8,128)(2,1)S(1)} %collective-permute-done.1), channel_id=1, source_target_pairs={{0,30},{2,0},{4,2},{6,4},{8,6},{10,8},{12,10},{14,12},{16,14},{18,... | collective-permute-start | bytes 15925256 | tf_op jit(solution)/shard_map/ppermute | solution.py:28
  133.8 341.6 %copy-start.7 = (bf16[9216,288]{0,1:T(8,128)(2,1)}, bf16[9216,288]{0,1:T(8,128)(2,1)S(1)}, u32[]{:S(2)}) copy-start(bf16[9216,288]{0,1:T(8,128)(2,1)S(1)} %collective-permute-done.2) | copy-start | bytes 15925252
  133.8 115.5 %collective-permute-start.4 = (bf16[9216,288]{0,1:T(8,128)(2,1)S(1)}, bf16[9216,288]{0,1:T(8,128)(2,1)S(1)}, u32[]{:S(2)}, u32[]{:S(2)}) collective-permute-start(bf16[9216,288]{0,1:T(8,128)(2,1)S(1)} %collective-permute-done.2), channel_id=1, source_target_pairs={{0,2},{2,4},{4,6},{6,8},{8,10},{10,12},{12,14},{14,16},{16,18},{18... | collective-permute-start | bytes 15925256 | tf_op jit(solution)/shard_map/ppermute | solution.py:20
  240.9 126.8 %copy-start.4 = (bf16[9216,288]{0,1:T(8,128)(2,1)}, bf16[9216,288]{0,1:T(8,128)(2,1)S(1)}, u32[]{:S(2)}) copy-start(bf16[9216,288]{0,1:T(8,128)(2,1)S(1)} %collective-permute-done.3) | copy-start | bytes 15925252
  240.9 118.3 %collective-permute-start.5 = (bf16[9216,288]{0,1:T(8,128)(2,1)S(1)}, bf16[9216,288]{0,1:T(8,128)(2,1)}, u32[]{:S(2)}, u32[]{:S(2)}) collective-permute-start(bf16[9216,288]{0,1:T(8,128)(2,1)S(1)} %collective-permute-done.3), channel_id=1, source_target_pairs={{0,30},{2,0},{4,2},{6,4},{8,6},{10,8},{12,10},{14,12},{16,14},{18,... | collective-permute-start | bytes 15925256 | tf_op jit(solution)/shard_map/ppermute | solution.py:28
  249.3 2.3 copy-start.3
  251.6 116.1 %collective-permute-start.6 = (bf16[9216,288]{0,1:T(8,128)(2,1)S(1)}, bf16[9216,288]{0,1:T(8,128)(2,1)}, u32[]{:S(2)}, u32[]{:S(2)}) collective-permute-start(bf16[9216,288]{0,1:T(8,128)(2,1)S(1)} %collective-permute-done.4), channel_id=1, source_target_pairs={{0,2},{2,4},{4,6},{6,8},{8,10},{10,12},{12,14},{14,16},{16,18},{18... | collective-permute-start | bytes 15925256 | tf_op jit(solution)/shard_map/ppermute | solution.py:20
  359.2 263.3 %collective-permute-start.7 = (bf16[9216,288]{0,1:T(8,128)(2,1)}, bf16[9216,288]{0,1:T(8,128)(2,1)}, u32[]{:S(2)}, u32[]{:S(2)}) collective-permute-start(bf16[9216,288]{0,1:T(8,128)(2,1)} %collective-permute-done.5), channel_id=1, source_target_pairs={{0,30},{2,0},{4,2},{6,4},{8,6},{10,8},{12,10},{14,12},{16,14},{18,... | collective-permute-start | bytes 15925256 | tf_op jit(solution)/shard_map/ppermute | solution.py:28
  367.8 273.1 %collective-permute-start.8 = (bf16[9216,288]{0,1:T(8,128)(2,1)}, bf16[9216,288]{0,1:T(8,128)(2,1)}, u32[]{:S(2)}, u32[]{:S(2)}) collective-permute-start(bf16[9216,288]{0,1:T(8,128)(2,1)} %collective-permute-done.6), channel_id=1, source_target_pairs={{0,2},{2,4},{4,6},{6,8},{8,10},{10,12},{12,14},{14,16},{16,18},{18... | collective-permute-start | bytes 15925256 | tf_op jit(solution)/shard_map/ppermute | solution.py:20
  551.0 67.2 %copy-start.8 = (f32[2304]{0:T(1024)S(1)}, f32[2304]{0:T(1024)}, u32[]{:S(2)}) copy-start(f32[2304]{0:T(1024)} %param.10) | copy-start | bytes 27652
  555.3 67.4 %copy-start.2 = (bf16[320,2304]{1,0:T(8,128)(2,1)S(1)}, bf16[320,2304]{1,0:T(8,128)(2,1)}, u32[]{:S(2)}) copy-start(bf16[320,2304]{1,0:T(8,128)(2,1)} %param.11) | copy-start | bytes 4423684
  622.6 63.1 %collective-permute-start.9 = (bf16[9216,288]{0,1:T(8,128)(2,1)}, bf16[9216,288]{0,1:T(8,128)(2,1)}, u32[]{:S(2)}, u32[]{:S(2)}) collective-permute-start(bf16[9216,288]{0,1:T(8,128)(2,1)} %collective-permute-done.7), channel_id=1, source_target_pairs={{0,30},{2,0},{4,2},{6,4},{8,6},{10,8},{12,10},{14,12},{16,14},{18,... | collective-permute-start | bytes 15925256 | tf_op jit(solution)/shard_map/ppermute | solution.py:28
  633.6 371.7 %reduce-scatter.12.cloned.1.call-start = ((), (), s32[]{:S(2)}) async-start(), calls=%async_computation.5 | async-start | bytes 5013504
  640.5 469.5 %reduce-scatter.8.cloned.1.call-start = ((), (), s32[]{:S(2)}) async-start(), calls=%async_computation.3 | async-start | bytes 8847360 | tf_op jit(solution)/shard_map/reduce_scatter | solution.py:58
  640.8 27.9 %slice-start = ((s8[5308416]{0:T(1024)(128)(4,1)}), s8[1114112]{0:T(1024)(128)(4,1)S(1)}, s32[]{:S(2)}) async-start(s8[5308416]{0:T(1024)(128)(4,1)} %bitcast.25), calls=%async_computation.6 | async-start | bytes 2228224
  640.8 27.9 %slice-start.1 = ((s8[5308416]{0:T(1024)(128)(4,1)}), s8[4194304]{0:T(1024)(128)(4,1)S(1)}, s32[]{:S(2)}) async-start(s8[5308416]{0:T(1024)(128)(4,1)} %bitcast.25), calls=%async_computation.7 | async-start | bytes 8388608
  640.8 67.7 %collective-permute-start.10 = (bf16[9216,288]{0,1:T(8,128)(2,1)}, bf16[9216,288]{0,1:T(8,128)(2,1)}, u32[]{:S(2)}, u32[]{:S(2)}) collective-permute-start(bf16[9216,288]{0,1:T(8,128)(2,1)} %collective-permute-done.8), channel_id=1, source_target_pairs={{0,2},{2,4},{4,6},{6,8},{8,10},{10,12},{12,14},{14,16},{16,18},{18... | collective-permute-start | bytes 15925256 | tf_op jit(solution)/shard_map/ppermute | solution.py:20
  671.4 11.2 slice-start.6
  671.4 17.2 %slice-start.4 = ((s8[5308416]{0:T(1024)(128)(4,1)}), s8[4194304]{0:T(1024)(128)(4,1)S(1)}, s32[]{:S(2)}) async-start(s8[5308416]{0:T(1024)(128)(4,1)} %bitcast.29), calls=%async_computation.10 | async-start | bytes 8388608
  677.1 5.5 slice-start.7
  677.1 11.5 slice-start.5
  682.6 109.2 %slice-start.2 = ((s8[5308416]{0:T(1024)(128)(4,1)}), s8[4194304]{0:T(1024)(128)(4,1)S(1)}, s32[]{:S(2)}) async-start(s8[5308416]{0:T(1024)(128)(4,1)} %bitcast.27), calls=%async_computation.8 | async-start | bytes 8388608
  685.7 106.1 %slice-start.3 = ((s8[5308416]{0:T(1024)(128)(4,1)}), s8[1114112]{0:T(1024)(128)(4,1)S(1)}, s32[]{:S(2)}) async-start(s8[5308416]{0:T(1024)(128)(4,1)} %bitcast.27), calls=%async_computation.9 | async-start | bytes 2228224
  685.7 124.4 %collective-permute-start.11 = (bf16[9216,288]{0,1:T(8,128)(2,1)}, bf16[9216,288]{0,1:T(8,128)(2,1)S(1)}, u32[]{:S(2)}, u32[]{:S(2)}) collective-permute-start(bf16[9216,288]{0,1:T(8,128)(2,1)} %collective-permute-done.9), channel_id=1, source_target_pairs={{0,30},{2,0},{4,2},{6,4},{8,6},{10,8},{12,10},{14,12},{16,14},{18,... | collective-permute-start | bytes 15925256 | tf_op jit(solution)/shard_map/ppermute | solution.py:28
  708.5 159.5 %collective-permute-start.12 = (bf16[9216,288]{0,1:T(8,128)(2,1)}, bf16[9216,288]{0,1:T(8,128)(2,1)S(1)}, u32[]{:S(2)}, u32[]{:S(2)}) collective-permute-start(bf16[9216,288]{0,1:T(8,128)(2,1)} %collective-permute-done.10), channel_id=1, source_target_pairs={{0,2},{2,4},{4,6},{6,8},{8,10},{10,12},{12,14},{14,16},{16,18},{18... | collective-permute-start | bytes 15925256 | tf_op jit(solution)/shard_map/ppermute | solution.py:20
  810.1 130.3 %collective-permute-start.13 = (bf16[9216,288]{0,1:T(8,128)(2,1)S(1)}, bf16[9216,288]{0,1:T(8,128)(2,1)S(1)}, u32[]{:S(2)}, u32[]{:S(2)}) collective-permute-start(bf16[9216,288]{0,1:T(8,128)(2,1)S(1)} %collective-permute-done.11), channel_id=1, source_target_pairs={{0,30},{2,0},{4,2},{6,4},{8,6},{10,8},{12,10},{14,12},{16,14},{18,... | collective-permute-start | bytes 15925256 | tf_op jit(solution)/shard_map/ppermute | solution.py:28
  868.0 90.6 %collective-permute-start.14 = (bf16[9216,288]{0,1:T(8,128)(2,1)S(1)}, bf16[9216,288]{0,1:T(8,128)(2,1)S(1)}, u32[]{:S(2)}, u32[]{:S(2)}) collective-permute-start(bf16[9216,288]{0,1:T(8,128)(2,1)S(1)} %collective-permute-done.12), channel_id=1, source_target_pairs={{0,2},{2,4},{4,6},{6,8},{8,10},{10,12},{12,14},{14,16},{16,18},{18... | collective-permute-start | bytes 15925256 | tf_op jit(solution)/shard_map/ppermute | solution.py:20
  1002.4 173.2 %copy-start.1 = (bf16[9216,16]{0,1:T(8,128)(2,1)S(1)}, bf16[9216,16]{0,1:T(8,128)(2,1)}, u32[]{:S(2)}) copy-start(bf16[9216,16]{0,1:T(8,128)(2,1)} %param.8) | copy-start | bytes 884740
Sparse Core Ops, SparseCore 0:
  633.8 137.6 reduce-scatter.9
  775.3 141.6 reduce-scatter.11
  1002.6 107.4 reduce-scatter.7
